TPU v7x, 32 devices: a whole 2x2x4 slice. The times are simulated.
32 devices in a mesh: section: 8 (over y, x, core), expert: 4 (over z).
Axes of the slice: x: 2, y: 2, z: 4, core: 2. Of those that a mesh axis runs over, the one named last changes fastest.
Arguments:
- top_grad: bfloat16 [2, 64, 2048], P(None, 'expert'), may hold values from -6 to 6
- layer_input: bfloat16 [8, 2, 64, 2048], P('section', None, 'expert'), may hold values from -6 to 6
- expert_out: bfloat16 [8, 2, 64, 2, 2048], P('section', None, 'expert'), may hold values from -3 to 3
- router_w: float32 [8, 2048, 8], P('section'), may hold values from -0.375 to 0.375
- expert_ids: int32 [8, 2, 64, 2], P('section', None, 'expert'), may hold values from 0 to 7, as said below
- hidden: bfloat16 [8, 2, 32, 7168], P('section', None, None, 'expert'), may hold values from -0.59765625 to 0.59765625
- down_w: bfloat16 [8, 7168, 2048], P('section', 'expert'), may hold values from -0.0625 to 0.0625
Outputs:
- input_grad: bfloat16 [8, 2, 64, 2048], P('section', None, 'expert')
- router_grad: float32 [8, 2048, 8], P('section')
- hidden_grad: bfloat16 [8, 2, 32, 7168], P('section', None, None, 'expert')
- down_grad: bfloat16 [8, 7168, 2048], P('section', 'expert')
Inputs may be any that keep to these rules, and one draw needn't show every extreme that they name: `expert_ids`: the two experts of a token differ. In each micro-batch, the 16 tokens of one device choose expert 0 at most 8 times, and exactly 8 times in some blocks of every draw.
All inputs are finite; a program needn't handle non-finite values.
Results may differ from a plain program's by a relative error of at most 0.024.
Values may be sent and summed in bfloat16 or wider, within the bound.
A program may use at most 64 MiB of HBM per device.

v0:
```python
import jax
import jax.numpy as jnp
from jax import lax
from jax.sharding import PartitionSpec as P


def passed_along(value, axis, by):
    count = lax.axis_size(axis)
    pairs = [(i, i + by) for i in range(count) if 0 <= i + by < count]
    return lax.ppermute(value, axis, pairs)


def gate_pair(inputs, weights, chosen):
    logits = jnp.einsum(
        "mtd,de->mte", inputs.astype(jnp.float32), weights, precision=lax.Precision.HIGHEST
    )
    select = (chosen[..., None] == jnp.arange(weights.shape[1], dtype=jnp.int32)).astype(
        jnp.float32
    )
    picked = jnp.sum(select * logits[..., None, :], axis=-1)
    gate_first = jax.nn.sigmoid(picked[..., 0] - picked[..., 1])
    return (gate_first, select)


def backprop(cotangent, inputs, outputs, weights, select, gate_first):
    cot_float = cotangent.astype(jnp.float32)
    gate_dot = jnp.einsum("mtkd,mtd->mtk", outputs, cotangent, preferred_element_type=jnp.float32)
    logit_diff = gate_first * (1.0 - gate_first) * (gate_dot[..., 0] - gate_dot[..., 1])
    logit_grad = logit_diff[..., None] * (select[..., 0, :] - select[..., 1, :])
    passed = cot_float + jnp.einsum(
        "mte,de->mtd", logit_grad, weights, precision=lax.Precision.HIGHEST
    )
    router_part = jnp.einsum(
        "mtd,mte->de", inputs.astype(jnp.float32), logit_grad, precision=lax.Precision.HIGHEST
    )
    return (passed.astype(jnp.bfloat16), router_part)


def dispatch_rows(cotangent, gate_first, chosen, capacity):
    is_zero = (chosen == 0).astype(jnp.float32)
    zero_gate = gate_first * is_zero[..., 0] + (1.0 - gate_first) * is_zero[..., 1]
    routed = is_zero[..., 0] + is_zero[..., 1]
    slot_pos = (jnp.cumsum(routed, axis=-1) - routed).astype(jnp.int32)
    slot_ids = jnp.arange(capacity, dtype=jnp.int32)
    pick_table = (
        (slot_pos[..., None, :] == slot_ids[:, None]) & (routed[..., None, :] > 0.5)
    ).astype(jnp.float32)
    scaled = zero_gate[..., None] * cotangent.astype(jnp.float32)
    rows_out = jnp.einsum("mbcu,mbud->mbcd", pick_table, scaled, precision=lax.Precision.HIGHEST)
    return rows_out.astype(jnp.bfloat16)


def per_device(top_grad, layer_input, expert_out, router_w, expert_ids, hidden, down_w):
    section_count = lax.axis_size("section")
    section_index = lax.axis_index("section")
    micro_count = top_grad.shape[0]
    tok_rows = top_grad.shape[1]
    width = top_grad.shape[2]
    inputs = layer_input[0]
    saved_outs = expert_out[0]
    router = router_w[0]
    chosen = expert_ids[0]
    gate_first, select = gate_pair(inputs, router, chosen)
    is_last = section_index == section_count - 1
    empty_cot = jnp.zeros((micro_count, tok_rows, width), jnp.bfloat16)
    empty_router = jnp.zeros((width, router.shape[1]), jnp.float32)

    def advance_all(moment, totals):
        arrived, section_dy, section_dx, router_acc = totals
        active = moment == section_count - 1 - section_index
        cotangent = jnp.where(is_last, top_grad, arrived)
        passed, router_part = backprop(cotangent, inputs, saved_outs, router, select, gate_first)
        section_dy = jnp.where(active, cotangent, section_dy)
        section_dx = jnp.where(active, passed, section_dx)
        router_acc = router_acc + jnp.where(active, router_part, 0.0)
        arrived = passed_along(passed, "section", -1)
        return (arrived, section_dy, section_dx, router_acc)

    start_state = (empty_cot, empty_cot, empty_cot, empty_router)
    _, section_dy, section_dx, router_acc = lax.fori_loop(
        0, section_count, advance_all, start_state
    )
    total_tokens = micro_count * tok_rows * lax.axis_size("expert")
    router_grad = lax.psum(router_acc, "expert") / total_tokens
    capacity = tok_rows // 2
    rows_out = dispatch_rows(section_dy[:, None], gate_first[:, None], chosen[:, None], capacity)
    rows_out = rows_out.reshape(micro_count, capacity, width)
    saved_hidden = hidden[0]
    weight = down_w[0]
    ff_local = weight.shape[0]
    slot_total = saved_hidden.shape[1]
    gathered = lax.all_gather(rows_out, "expert", axis=1, tiled=True)
    flat_rows = gathered.reshape(-1, width)
    hidden_acc = lax.dot_general(
        flat_rows, weight, (((1,), (1,)), ((), ())), preferred_element_type=jnp.float32
    )
    hidden_acc = hidden_acc.astype(jnp.bfloat16).reshape(micro_count, slot_total, ff_local)
    weight_sum = lax.dot_general(
        saved_hidden.reshape(-1, ff_local),
        flat_rows,
        (((0,), (0,)), ((), ())),
        preferred_element_type=jnp.float32,
    )
    return (
        section_dx[None],
        router_grad[None],
        hidden_acc[None],
        weight_sum.astype(jnp.bfloat16)[None],
    )


def solution(mesh):
    placed = (
        P(None, "expert", None),
        P("section", None, "expert", None),
        P("section", None, "expert", None, None),
        P("section", None, None),
        P("section", None, "expert", None),
        P("section", None, None, "expert"),
        P("section", "expert", None),
    )
    return jax.shard_map(
        per_device,
        mesh=mesh,
        in_specs=placed,
        out_specs=(
            P("section", None, "expert", None),
            P("section", None, None),
            P("section", None, None, "expert"),
            P("section", "expert", None),
        ),
        check_vma=False,
    )
```

profile of v0, /device:TPU:0, one launch (start us, length us, event | category | flops | bytes accessed | tf_op | source)
XLA Modules:
  0.0 136.3 jit_solution(297032122991663004)
XLA Ops:
  8.0 1.5 %fusion.22 = f32[2,16,8]{1,2,0:T(8,128)S(1)} fusion(f32[1,2048,8]{1,2,0:T(8,128)} %param.12, bf16[1,2,16,2048]{3,2,1,0:T(8,128)(2,1)} %param.10), kind=kOutput, calls=%fused_computation.29 | convolution fusion | flops 6291456 | bytes 197632 | tf_op jit(solution)/shard_map/mtd,de->mte/dot_general | solution.py:14
  9.5 73.4 %while.22 = (s32[]{:T(128)}, bf16[2,16,2048]{2,1,0:T(8,128)(2,1)S(1)}, bf16[2,16,2048]{2,1,0:T(8,128)(2,1)S(1)}, bf16[2,16,2048]{2,1,0:T(8,128)(2,1)S(1)}, f32[2...) while((s32[]{:T(128)}, ...), condition=%wide.region_2.3_spmd.clone, body=%wide.region_1.2_spmd.clone.sunk | while | flops 13419140 | bytes 2428622 | solution.py:80
  9.7 1.6 %fusion.53 = f32[2,16,1,2]{3,2,1,0:T(1,128)S(1)} fusion(bf16[2,16,2,2048]{3,2,1,0:T(2,128)(2,1)} %get-tuple-element.510, bf16[2,16,2048,1]{2,1,0,3:T(8,128)(2,1)S(1)} %bitcast.83), kind=kOutput, calls=%fused_computation.6.clone.1 | convolution fusion | flops 262144 | bytes 393472 | tf_op jit(solution)/shard_map/while/body/eval_jaxpr/mtkd,mtd->mtk/dot_general | solution.py:27
  11.3 1.3 select_select_fusion.5
  12.6 1.3 collective-permute-start
  13.9 1.1 fusion.55
  15.1 0.8 collective-permute-done
  15.9 1.6 %fusion.53 = f32[2,16,1,2]{3,2,1,0:T(1,128)S(1)} fusion(bf16[2,16,2,2048]{3,2,1,0:T(2,128)(2,1)} %get-tuple-element.510, bf16[2,16,2048,1]{2,1,0,3:T(8,128)(2,1)S(1)} %bitcast.83), kind=kOutput, calls=%fused_computation.6.clone.1 | convolution fusion | flops 262144 | bytes 393472 | tf_op jit(solution)/shard_map/while/body/eval_jaxpr/mtkd,mtd->mtk/dot_general | solution.py:27
  17.6 1.3 select_select_fusion.5
  18.9 1.3 collective-permute-start
  20.2 1.1 fusion.55
  21.4 4.7 %collective-permute-done = bf16[2,16,2048]{2,1,0:T(8,128)(2,1)S(1)} collective-permute-done((bf16[2,16,2048]{2,1,0:T(8,128)(2,1)S(1)}, bf16[2,16,2048]{2,1,0:T(8,128)(2,1)S(1)}, u32[]{:S(2)}, u32[]{:S(2)}) %collective-permute-start) | collective-permute-done | bytes 131104 | tf_op jit(solution)/shard_map/while/body/eval_jaxpr/ppermute | solution.py:10
  26.1 1.6 %fusion.53 = f32[2,16,1,2]{3,2,1,0:T(1,128)S(1)} fusion(bf16[2,16,2,2048]{3,2,1,0:T(2,128)(2,1)} %get-tuple-element.510, bf16[2,16,2048,1]{2,1,0,3:T(8,128)(2,1)S(1)} %bitcast.83), kind=kOutput, calls=%fused_computation.6.clone.1 | convolution fusion | flops 262144 | bytes 393472 | tf_op jit(solution)/shard_map/while/body/eval_jaxpr/mtkd,mtd->mtk/dot_general | solution.py:27
  27.8 1.3 select_select_fusion.5
  29.1 1.3 collective-permute-start
  30.4 1.1 fusion.55
  31.6 3.8 %collective-permute-done = bf16[2,16,2048]{2,1,0:T(8,128)(2,1)S(1)} collective-permute-done((bf16[2,16,2048]{2,1,0:T(8,128)(2,1)S(1)}, bf16[2,16,2048]{2,1,0:T(8,128)(2,1)S(1)}, u32[]{:S(2)}, u32[]{:S(2)}) %collective-permute-start) | collective-permute-done | bytes 131104 | tf_op jit(solution)/shard_map/while/body/eval_jaxpr/ppermute | solution.py:10
  35.5 1.6 %fusion.53 = f32[2,16,1,2]{3,2,1,0:T(1,128)S(1)} fusion(bf16[2,16,2,2048]{3,2,1,0:T(2,128)(2,1)} %get-tuple-element.510, bf16[2,16,2048,1]{2,1,0,3:T(8,128)(2,1)S(1)} %bitcast.83), kind=kOutput, calls=%fused_computation.6.clone.1 | convolution fusion | flops 262144 | bytes 393472 | tf_op jit(solution)/shard_map/while/body/eval_jaxpr/mtkd,mtd->mtk/dot_general | solution.py:27
  37.2 1.3 select_select_fusion.5
  38.5 1.3 collective-permute-start
  39.8 1.1 fusion.55
  40.9 3.8 %collective-permute-done = bf16[2,16,2048]{2,1,0:T(8,128)(2,1)S(1)} collective-permute-done((bf16[2,16,2048]{2,1,0:T(8,128)(2,1)S(1)}, bf16[2,16,2048]{2,1,0:T(8,128)(2,1)S(1)}, u32[]{:S(2)}, u32[]{:S(2)}) %collective-permute-start) | collective-permute-done | bytes 131104 | tf_op jit(solution)/shard_map/while/body/eval_jaxpr/ppermute | solution.py:10
  44.8 1.6 %fusion.53 = f32[2,16,1,2]{3,2,1,0:T(1,128)S(1)} fusion(bf16[2,16,2,2048]{3,2,1,0:T(2,128)(2,1)} %get-tuple-element.510, bf16[2,16,2048,1]{2,1,0,3:T(8,128)(2,1)S(1)} %bitcast.83), kind=kOutput, calls=%fused_computation.6.clone.1 | convolution fusion | flops 262144 | bytes 393472 | tf_op jit(solution)/shard_map/while/body/eval_jaxpr/mtkd,mtd->mtk/dot_general | solution.py:27
  46.5 1.3 select_select_fusion.5
  47.8 1.3 collective-permute-start
  49.1 1.1 fusion.55
  50.3 3.8 %collective-permute-done = bf16[2,16,2048]{2,1,0:T(8,128)(2,1)S(1)} collective-permute-done((bf16[2,16,2048]{2,1,0:T(8,128)(2,1)S(1)}, bf16[2,16,2048]{2,1,0:T(8,128)(2,1)S(1)}, u32[]{:S(2)}, u32[]{:S(2)}) %collective-permute-start) | collective-permute-done | bytes 131104 | tf_op jit(solution)/shard_map/while/body/eval_jaxpr/ppermute | solution.py:10
  54.2 1.6 %fusion.53 = f32[2,16,1,2]{3,2,1,0:T(1,128)S(1)} fusion(bf16[2,16,2,2048]{3,2,1,0:T(2,128)(2,1)} %get-tuple-element.510, bf16[2,16,2048,1]{2,1,0,3:T(8,128)(2,1)S(1)} %bitcast.83), kind=kOutput, calls=%fused_computation.6.clone.1 | convolution fusion | flops 262144 | bytes 393472 | tf_op jit(solution)/shard_map/while/body/eval_jaxpr/mtkd,mtd->mtk/dot_general | solution.py:27
  55.9 1.3 select_select_fusion.5
  57.2 1.3 collective-permute-start
  58.5 1.1 fusion.55
  59.6 3.8 %collective-permute-done = bf16[2,16,2048]{2,1,0:T(8,128)(2,1)S(1)} collective-permute-done((bf16[2,16,2048]{2,1,0:T(8,128)(2,1)S(1)}, bf16[2,16,2048]{2,1,0:T(8,128)(2,1)S(1)}, u32[]{:S(2)}, u32[]{:S(2)}) %collective-permute-start) | collective-permute-done | bytes 131104 | tf_op jit(solution)/shard_map/while/body/eval_jaxpr/ppermute | solution.py:10
  63.5 1.6 %fusion.53 = f32[2,16,1,2]{3,2,1,0:T(1,128)S(1)} fusion(bf16[2,16,2,2048]{3,2,1,0:T(2,128)(2,1)} %get-tuple-element.510, bf16[2,16,2048,1]{2,1,0,3:T(8,128)(2,1)S(1)} %bitcast.83), kind=kOutput, calls=%fused_computation.6.clone.1 | convolution fusion | flops 262144 | bytes 393472 | tf_op jit(solution)/shard_map/while/body/eval_jaxpr/mtkd,mtd->mtk/dot_general | solution.py:27
  65.2 1.3 select_select_fusion.5
  66.5 1.3 collective-permute-start
  67.8 1.1 fusion.55
  69.0 3.8 %collective-permute-done = bf16[2,16,2048]{2,1,0:T(8,128)(2,1)S(1)} collective-permute-done((bf16[2,16,2048]{2,1,0:T(8,128)(2,1)S(1)}, bf16[2,16,2048]{2,1,0:T(8,128)(2,1)S(1)}, u32[]{:S(2)}, u32[]{:S(2)}) %collective-permute-start) | collective-permute-done | bytes 131104 | tf_op jit(solution)/shard_map/while/body/eval_jaxpr/ppermute | solution.py:10
  72.9 1.6 %fusion.53 = f32[2,16,1,2]{3,2,1,0:T(1,128)S(1)} fusion(bf16[2,16,2,2048]{3,2,1,0:T(2,128)(2,1)} %get-tuple-element.510, bf16[2,16,2048,1]{2,1,0,3:T(8,128)(2,1)S(1)} %bitcast.83), kind=kOutput, calls=%fused_computation.6.clone.1 | convolution fusion | flops 262144 | bytes 393472 | tf_op jit(solution)/shard_map/while/body/eval_jaxpr/mtkd,mtd->mtk/dot_general | solution.py:27
  74.6 1.3 select_select_fusion.5
  75.9 1.3 collective-permute-start
  77.2 1.1 fusion.55
  78.3 4.6 %collective-permute-done = bf16[2,16,2048]{2,1,0:T(8,128)(2,1)S(1)} collective-permute-done((bf16[2,16,2048]{2,1,0:T(8,128)(2,1)S(1)}, bf16[2,16,2048]{2,1,0:T(8,128)(2,1)S(1)}, u32[]{:S(2)}, u32[]{:S(2)}) %collective-permute-start) | collective-permute-done | bytes 131104 | tf_op jit(solution)/shard_map/while/body/eval_jaxpr/ppermute | solution.py:10
  84.2 14.3 %all_gather.3 = bf16[2,32,2048]{2,1,0:T(8,128)(2,1)S(1)} all-gather(bf16[2,8,2048]{2,1,0:T(8,128)(2,1)S(1)} %convolution_convert_fusion.1), channel_id=1, replica_groups=mesh['section'=8,'expert'=4] {'expert'}, dimensions={1}, use_global_device_ids=true | all-gather | bytes 327680 | tf_op jit(solution)/shard_map/all_gather | solution.py:92
  98.4 6.1 %fusion.16 = bf16[64,1792]{1,0:T(8,128)(2,1)} fusion(bf16[64,2048]{1,0:T(8,128)(2,1)S(1)} %bitcast.85, bf16[1,1792,2048]{2,1,0:T(8,128)(2,1)} %param.15), kind=kOutput, calls=%fused_computation.24 | convolution fusion | flops 469876736 | bytes 7831552 | tf_op jit(solution)/shard_map/dot_general | solution.py:94
  104.5 5.1 %fusion.15 = bf16[1,1792,2048]{1,2,0:T(8,128)(2,1)} fusion(bf16[64,2048]{1,0:T(8,128)(2,1)S(1)} %bitcast.86, bf16[64,1792]{1,0:T(8,128)(2,1)S(1)} %bitcast.82), kind=kOutput, calls=%fused_computation.23 | convolution fusion | flops 473432064 | bytes 7831552 | tf_op jit(solution)/shard_map/dot_general | solution.py:98
  109.6 10.4 %copy.14 = bf16[1,1792,2048]{2,1,0:T(8,128)(2,1)} copy(bf16[1,1792,2048]{1,2,0:T(8,128)(2,1)} %fusion.15) | data formatting | bytes 14680064
  120.1 7.9 %all-reduce.2.cloned.1.call-done = f32[2048,8]{0,1:T(8,128)} async-done(((f32[2048,8]{0,1:T(8,128)}), f32[2048,8]{0,1:T(8,128)}) %all-reduce.2.cloned.1.call-update) | async-done | bytes 65552 | tf_op jit(solution)/shard_map/psum | solution.py:84
  128.0 1.5 %multiply_bitcast_fusion = f32[1,2048,8]{1,2,0:T(8,128)} fusion(f32[2048,8]{0,1:T(8,128)} %all-reduce.2.cloned.1.call-done), kind=kLoop, calls=%fused_computation.31 | loop fusion | flops 16384 | bytes 131072 | tf_op jit(solution)/shard_map/broadcast_in_dim | solution.py:106
  (50 shorter events, 3.3 us)
Async XLA Ops:
  7.2 97.4 %copy-start = (bf16[1,2,32,1792]{3,2,1,0:T(8,128)(2,1)S(1)}, bf16[1,2,32,1792]{3,2,1,0:T(8,128)(2,1)}, u32[]{:S(2)}) copy-start(bf16[1,2,32,1792]{3,2,1,0:T(8,128)(2,1)} %param.14) | copy-start | bytes 688132
  7.2 120.8 %all-reduce.2.cloned.1.call-start = ((), (), s32[]{:S(2)}) async-start(), calls=%async_computation | async-start | bytes 131072 | tf_op jit(solution)/shard_map/psum | solution.py:84
  9.5 74.1 %copy-start.3 = (s32[1,2,16,2]{2,3,1,0:T(2,128)S(1)}, s32[1,2,16,2]{2,3,1,0:T(2,128)}, u32[]{:S(2)}) copy-start(s32[1,2,16,2]{2,3,1,0:T(2,128)} %param.13) | copy-start | bytes 772
  12.6 3.2 %collective-permute-start = (bf16[2,16,2048]{2,1,0:T(8,128)(2,1)S(1)}, bf16[2,16,2048]{2,1,0:T(8,128)(2,1)S(1)}, u32[]{:S(2)}, u32[]{:S(2)}) collective-permute-start(bf16[2,16,2048]{2,1,0:T(8,128)(2,1)S(1)} %get-tuple-element.469), channel_id=1, source_target_pairs={{4,0},{8,4},{12,8},{16,12},{20,16},{24,20},{28,24},{5,1},{9,5},{13... | collective-permute-start | bytes 393224 | tf_op jit(solution)/shard_map/while/body/eval_jaxpr/ppermute | solution.py:10
  18.9 7.2 %collective-permute-start = (bf16[2,16,2048]{2,1,0:T(8,128)(2,1)S(1)}, bf16[2,16,2048]{2,1,0:T(8,128)(2,1)S(1)}, u32[]{:S(2)}, u32[]{:S(2)}) collective-permute-start(bf16[2,16,2048]{2,1,0:T(8,128)(2,1)S(1)} %get-tuple-element.469), channel_id=1, source_target_pairs={{4,0},{8,4},{12,8},{16,12},{20,16},{24,20},{28,24},{5,1},{9,5},{13... | collective-permute-start | bytes 393224 | tf_op jit(solution)/shard_map/while/body/eval_jaxpr/ppermute | solution.py:10
  29.1 6.3 %collective-permute-start = (bf16[2,16,2048]{2,1,0:T(8,128)(2,1)S(1)}, bf16[2,16,2048]{2,1,0:T(8,128)(2,1)S(1)}, u32[]{:S(2)}, u32[]{:S(2)}) collective-permute-start(bf16[2,16,2048]{2,1,0:T(8,128)(2,1)S(1)} %get-tuple-element.469), channel_id=1, source_target_pairs={{4,0},{8,4},{12,8},{16,12},{20,16},{24,20},{28,24},{5,1},{9,5},{13... | collective-permute-start | bytes 393224 | tf_op jit(solution)/shard_map/while/body/eval_jaxpr/ppermute | solution.py:10
  38.5 6.3 %collective-permute-start = (bf16[2,16,2048]{2,1,0:T(8,128)(2,1)S(1)}, bf16[2,16,2048]{2,1,0:T(8,128)(2,1)S(1)}, u32[]{:S(2)}, u32[]{:S(2)}) collective-permute-start(bf16[2,16,2048]{2,1,0:T(8,128)(2,1)S(1)} %get-tuple-element.469), channel_id=1, source_target_pairs={{4,0},{8,4},{12,8},{16,12},{20,16},{24,20},{28,24},{5,1},{9,5},{13... | collective-permute-start | bytes 393224 | tf_op jit(solution)/shard_map/while/body/eval_jaxpr/ppermute | solution.py:10
  47.8 6.3 %collective-permute-start = (bf16[2,16,2048]{2,1,0:T(8,128)(2,1)S(1)}, bf16[2,16,2048]{2,1,0:T(8,128)(2,1)S(1)}, u32[]{:S(2)}, u32[]{:S(2)}) collective-permute-start(bf16[2,16,2048]{2,1,0:T(8,128)(2,1)S(1)} %get-tuple-element.469), channel_id=1, source_target_pairs={{4,0},{8,4},{12,8},{16,12},{20,16},{24,20},{28,24},{5,1},{9,5},{13... | collective-permute-start | bytes 393224 | tf_op jit(solution)/shard_map/while/body/eval_jaxpr/ppermute | solution.py:10
  57.2 6.3 %collective-permute-start = (bf16[2,16,2048]{2,1,0:T(8,128)(2,1)S(1)}, bf16[2,16,2048]{2,1,0:T(8,128)(2,1)S(1)}, u32[]{:S(2)}, u32[]{:S(2)}) collective-permute-start(bf16[2,16,2048]{2,1,0:T(8,128)(2,1)S(1)} %get-tuple-element.469), channel_id=1, source_target_pairs={{4,0},{8,4},{12,8},{16,12},{20,16},{24,20},{28,24},{5,1},{9,5},{13... | collective-permute-start | bytes 393224 | tf_op jit(solution)/shard_map/while/body/eval_jaxpr/ppermute | solution.py:10
  66.5 6.3 %collective-permute-start = (bf16[2,16,2048]{2,1,0:T(8,128)(2,1)S(1)}, bf16[2,16,2048]{2,1,0:T(8,128)(2,1)S(1)}, u32[]{:S(2)}, u32[]{:S(2)}) collective-permute-start(bf16[2,16,2048]{2,1,0:T(8,128)(2,1)S(1)} %get-tuple-element.469), channel_id=1, source_target_pairs={{4,0},{8,4},{12,8},{16,12},{20,16},{24,20},{28,24},{5,1},{9,5},{13... | collective-permute-start | bytes 393224 | tf_op jit(solution)/shard_map/while/body/eval_jaxpr/ppermute | solution.py:10
  75.9 7.1 %collective-permute-start = (bf16[2,16,2048]{2,1,0:T(8,128)(2,1)S(1)}, bf16[2,16,2048]{2,1,0:T(8,128)(2,1)S(1)}, u32[]{:S(2)}, u32[]{:S(2)}) collective-permute-start(bf16[2,16,2048]{2,1,0:T(8,128)(2,1)S(1)} %get-tuple-element.469), channel_id=1, source_target_pairs={{4,0},{8,4},{12,8},{16,12},{20,16},{24,20},{28,24},{5,1},{9,5},{13... | collective-permute-start | bytes 393224 | tf_op jit(solution)/shard_map/while/body/eval_jaxpr/ppermute | solution.py:10
  82.9 0.6 copy-start.2
  82.9 26.7 %copy-start.1 = (bf16[2,16,2048]{2,1,0:T(8,128)(2,1)}, bf16[2,16,2048]{2,1,0:T(8,128)(2,1)S(1)}, u32[]{:S(2)}) copy-start(bf16[2,16,2048]{2,1,0:T(8,128)(2,1)S(1)} %get-tuple-element.304) | copy-start | bytes 393220
Sparse Core Ops, SparseCore 0:
  83.7 44.2 all-reduce.1
where the time goes:
time: 138 us; the launch traced here: 136 us
  matrix products  45.1 us (33%)
  waiting for transfers between devices  37.2 us (27%)
  blocking collectives  14.3 us (10%)
  between operations  14.2 us (10%)
  local copies, waits for them, and re-layouts  12.5 us (9%)
  starting transfers between devices  10.4 us (8%)
  other arithmetic  2.4 us (2%)
    ppermute x8, waiting for transfers between devices, passed_along(): return lax.ppermute(value, axis, pairs)  29.3 us
    all_gather x1, blocking collectives, per_device(): gathered = lax.all_gather(rows_out, 'expert', axis=1, tiled=True)  14.3 us
    dot_general x8, matrix products, backprop(): jnp.einsum('mtkd,mtd->mtk', outputs, cotangent, preferred_element_type=jn...  12.8 us
    unnamed x9, local copies, waits for them, and re-layouts  11.1 us
    ppermute x8, starting transfers between devices, passed_along(): return lax.ppermute(value, axis, pairs)  10.3 us
    dot_general x8, matrix products, backprop(): jnp.einsum('mte,de->mtd', logit_grad, weights, precision=lax.Precision.HI...  10.3 us
    dot_general x8, matrix products, backprop(): jnp.einsum('mtd,mte->de', inputs.astype(jnp.float32), logit_grad, precisi...  9.18 us
    psum x1, waiting for transfers between devices, per_device(): router_grad = lax.psum(router_acc, 'expert') / total_tokens  7.93 us
  transfers between devices with their start and end apart: 9, of which 9 were waited for; matrix products, arithmetic and copies ran while one was open for 23% of the time, Pallas kernels for 0%

commit v1 on v0

v1 whole, which is shorter than its diff:
```python
import functools

import jax
import jax.numpy as jnp
from jax import lax
from jax.experimental import pallas as pl
from jax.experimental.pallas import tpu as pltpu
from jax.sharding import PartitionSpec as P

F32 = jnp.float32
BF16 = jnp.bfloat16
MESH = pl.DeviceIdType.MESH


def iota(shape, axis):
    return lax.broadcasted_iota(jnp.int32, shape, axis)


def dot(a, b, dims=((1,), (0,)), precision=None):
    return lax.dot_general(a, b, (dims, ((), ())), preferred_element_type=F32, precision=precision)


def push(src, dst, send, recv, axis, target):
    return pltpu.make_async_remote_copy(
        src_ref=src,
        dst_ref=dst,
        send_sem=send,
        recv_sem=recv,
        device_id={axis: target},
        device_id_type=MESH,
    )


def chain_kernel(
    sections,
    parts,
    top_ref,
    x_ref,
    outs_ref,
    w_ref,
    ids_ref,
    dx_ref,
    router_ref,
    rows_ref,
    wsend,
    wbuf,
    tsend,
    tbuf,
    zsend,
    zbuf,
    msend,
    mbuf,
    psend,
    pbuf,
    w_out,
    w_in,
    t_out,
    t_in,
    z_out,
    z_in,
    m_out,
    m_in,
    p_out,
    p_in,
):
    me = lax.axis_index("section")
    spot = lax.axis_index("expert")
    experts, width = w_ref.shape
    micro, tok = ids_ref.shape[0], ids_ref.shape[2]
    tokens = micro * tok
    cap = tok // 2
    slots = micro * cap
    lanes = wsend.shape[1] - width
    all_rows = sections * experts
    pad = msend.shape[1] - all_rows

    barrier = pltpu.get_barrier_semaphore()
    for i in range(1, sections):
        pl.semaphore_signal(
            barrier, inc=1, device_id={"section": (me + i) % sections}, device_id_type=MESH
        )
    for i in range(1, parts):
        pl.semaphore_signal(
            barrier, inc=1, device_id={"expert": (spot + i) % parts}, device_id_type=MESH
        )

    weights = w_ref[...]
    high = weights.astype(BF16)
    low = weights - high.astype(F32)
    sel_wide = jnp.zeros((experts, lanes), F32)
    for m in range(micro):
        ids = ids_ref[m]
        kind = iota((experts, tok), 0)
        one_hot = (ids[0:1, :] == kind).astype(F32) - (ids[1:2, :] == kind).astype(F32)
        place = (iota((tok, lanes), 0) + m * tok == iota((tok, lanes), 1)).astype(BF16)
        sel_wide = sel_wide + dot(one_hot.astype(BF16), place)
    wsend[:, :width] = high
    wsend[:, width:] = sel_wide.astype(BF16)
    wbuf[me, :, :width] = high
    wbuf[me, :, width:] = sel_wide.astype(BF16)

    pl.semaphore_wait(barrier, sections + parts - 2)
    sends = []

    def spread(src, buf, out_sem, in_sem, axis, mine, count):
        for i in range(1, count):
            target = (mine + i) % count
            copy = push(src, buf.at[mine], out_sem.at[i], in_sem.at[mine], axis, target)
            copy.start()
            sends.append(copy)

    def collect(src, buf, out_sem, in_sem, axis, mine, count):
        for i in range(1, count):
            source = (mine + i) % count
            push(src, buf.at[source], out_sem.at[i], in_sem.at[source], axis, source).wait_recv()

    spread(wsend, wbuf, w_out, w_in, "section", me, sections)

    sel = sel_wide[:, :tokens]
    first = sel[0:1, :]
    routed = jnp.abs(first)
    before = (
        (iota((tokens, tokens), 0) // tok == iota((tokens, tokens), 1) // tok)
        & (iota((tokens, tokens), 0) < iota((tokens, tokens), 1))
    ).astype(BF16)
    spots = dot(jnp.broadcast_to(routed, (8, tokens)).astype(BF16), before)[0:1, :]
    slot_row = iota((slots, tokens), 0)
    slot_table = (
        (slot_row // cap == iota((slots, tokens), 1) // tok)
        & (spots.astype(jnp.int32) == slot_row % cap)
        & (routed > 0.5)
    ).astype(F32)
    top = top_ref[...].reshape(tokens, width)
    top_rows = dot(slot_table.astype(BF16), top).astype(BF16)
    tsend[...] = top_rows
    tbuf[spot] = top_rows
    spread(tsend, tbuf, t_out, t_in, "expert", spot, parts)

    x = x_ref[...].reshape(tokens, width)
    both = jnp.concatenate([high.astype(F32), low], axis=0).astype(BF16)
    logits = dot(both, x, ((1,), (1,)))
    logits = logits[:experts] + logits[experts:]
    gate = 1.0 / (1.0 + jnp.exp(-jnp.sum(sel * logits, axis=0, keepdims=True)))
    slope = gate * (1.0 - gate)
    gate_zero = jnp.where(first > 0.5, gate, 1.0 - gate)
    gated_table = slot_table * gate_zero

    diff = (outs_ref[:, 0, :].astype(F32) - outs_ref[:, 1, :].astype(F32)).astype(BF16)
    eye = (iota((tokens, tokens), 0) == iota((tokens, tokens), 1)).astype(F32)
    base = jnp.sum(dot(top, diff, ((1,), (1,))) * eye, axis=0, keepdims=True)

    collect(wsend, wbuf, w_out, w_in, "section", me, sections)
    wall = jnp.concatenate(
        [wbuf[k, :, :width].astype(F32) for k in range(sections)], axis=0
    ).astype(BF16)
    sel_all = jnp.concatenate(
        [wbuf[k, :, width : width + tokens].astype(F32) for k in range(sections)], axis=0
    )
    cross = dot(wall, diff, ((1,), (1,))) * sel_all
    cross = jnp.sum(cross.reshape(sections, experts, tokens), axis=1)
    layer = iota((sections, tokens), 0)
    terms = slope * jnp.where(layer > me, cross, jnp.where(layer == me, base, 0.0))
    zsend[:, :tokens] = terms
    zbuf[me, :, :tokens] = terms
    spread(zsend, zbuf, z_out, z_in, "section", me, sections)
    collect(zsend, zbuf, z_out, z_in, "section", me, sections)

    steps = jnp.zeros((sections, tokens), F32)
    for j in range(sections - 1, -1, -1):
        line = zbuf[j, :, :tokens]
        value = jnp.sum(jnp.where(layer == j, line, line * steps), axis=0, keepdims=True)
        steps = jnp.where(layer == j, value, steps)

    spread_steps = jnp.broadcast_to(
        steps.reshape(sections, 1, tokens), (sections, experts, tokens)
    ).reshape(all_rows, tokens)
    coefs = sel_all * spread_steps
    owner = iota((all_rows, tokens), 0) // experts
    above = jnp.where(owner > me, coefs, 0.0)
    stacked = jnp.concatenate([above, jnp.ones((pad, tokens), F32)], axis=0)
    mix = dot(gated_table, stacked, ((1,), (1,)), lax.Precision.HIGHEST)
    msend[...] = mix
    mbuf[spot] = mix
    spread(msend, mbuf, m_out, m_in, "expert", spot, parts)

    own = sel * jnp.sum(jnp.where(layer == me, steps, 0.0), axis=0, keepdims=True)
    own_high = own.astype(BF16).astype(F32)
    own_both = jnp.concatenate([own_high, own - own_high], axis=0).astype(BF16)
    share = dot(own_both, x)
    share = (share[:experts] + share[experts:]) * (1.0 / (tokens * parts))
    psend[...] = share.astype(BF16)
    spread(psend, pbuf, p_out, p_in, "expert", spot, parts)

    upto = jnp.where(owner >= me, coefs, 0.0).astype(BF16)
    moved = top.astype(F32) + dot(upto, wall, ((0,), (0,)))
    dx_ref[...] = moved.astype(BF16).reshape(dx_ref.shape)

    collect(tsend, tbuf, t_out, t_in, "expert", spot, parts)
    collect(msend, mbuf, m_out, m_in, "expert", spot, parts)
    for e in range(parts):
        mixed = mbuf[e]
        part = dot(mixed[:, :all_rows].astype(BF16), wall)
        part = part + mixed[:, all_rows : all_rows + 1] * tbuf[e].astype(F32)
        for m in range(micro):
            rows_ref[m, e * cap : (e + 1) * cap, :] = part[m * cap : (m + 1) * cap].astype(BF16)

    collect(psend, pbuf, p_out, p_in, "expert", spot, parts)
    total = share
    for i in range(1, parts):
        total = total + pbuf[(spot + i) % parts].astype(F32)
    router_ref[...] = total
    for copy in sends:
        copy.wait_send()


def expert_kernel(rows_ref, hidden_ref, weight_ref, hidden_out, weight_out):
    rows = rows_ref[...]
    hidden_out[...] = dot(rows, weight_ref[...], ((1,), (1,))).astype(BF16)
    weight_out[...] = dot(hidden_ref[...], rows, ((0,), (0,))).astype(BF16)


def per_device(top_grad, layer_input, expert_out, router_w, expert_ids, hidden, down_w):
    sections = lax.axis_size("section")
    parts = lax.axis_size("expert")
    micro, tok, width = top_grad.shape
    experts = router_w.shape[2]
    tokens = micro * tok
    cap = tok // 2
    slots = micro * cap
    lanes = -(-tokens // 128) * 128
    mix_lanes = (sections * experts // 128 + 1) * 128
    vmem = pl.BlockSpec(memory_space=pltpu.VMEM)
    dma = pltpu.SemaphoreType.DMA
    section_dx, router_grad, rows = pl.pallas_call(
        functools.partial(chain_kernel, sections, parts),
        out_shape=(
            jax.ShapeDtypeStruct((micro, tok, width), BF16),
            jax.ShapeDtypeStruct((experts, width), F32),
            jax.ShapeDtypeStruct((micro, parts * cap, width), BF16),
        ),
        in_specs=[vmem] * 5,
        out_specs=(vmem,) * 3,
        scratch_shapes=[
            pltpu.VMEM((experts, width + lanes), BF16),
            pltpu.VMEM((sections, experts, width + lanes), BF16),
            pltpu.VMEM((slots, width), BF16),
            pltpu.VMEM((parts, slots, width), BF16),
            pltpu.VMEM((sections, lanes), F32),
            pltpu.VMEM((sections, sections, lanes), F32),
            pltpu.VMEM((slots, mix_lanes), F32),
            pltpu.VMEM((parts, slots, mix_lanes), F32),
            pltpu.VMEM((experts, width), BF16),
            pltpu.VMEM((parts, experts, width), BF16),
            dma((sections,)),
            dma((sections,)),
            dma((parts,)),
            dma((parts,)),
            dma((sections,)),
            dma((sections,)),
            dma((parts,)),
            dma((parts,)),
            dma((parts,)),
            dma((parts,)),
        ],
        compiler_params=pltpu.CompilerParams(
            collective_id=0, has_side_effects=True, vmem_limit_bytes=24 * 1024 * 1024
        ),
        cost_estimate=pl.CostEstimate(flops=10**9, bytes_accessed=4 * 10**7, transcendentals=0),
        name="chain",
    )(
        top_grad,
        layer_input[0],
        expert_out[0].reshape(tokens, 2, width),
        jnp.swapaxes(router_w[0], 0, 1),
        jnp.swapaxes(expert_ids[0], 1, 2),
    )
    flat_rows = rows.reshape(-1, width)
    saved = hidden[0]
    ff = down_w.shape[1]
    slot_total = flat_rows.shape[0]
    tile = 256 if ff % 256 == 0 else (128 if ff % 128 == 0 else ff)
    hidden_grad, down_grad = pl.pallas_call(
        expert_kernel,
        grid=(ff // tile,),
        out_shape=(
            jax.ShapeDtypeStruct((slot_total, ff), BF16),
            jax.ShapeDtypeStruct((ff, width), BF16),
        ),
        in_specs=[
            pl.BlockSpec((slot_total, width), lambda i: (0, 0)),
            pl.BlockSpec((slot_total, tile), lambda i: (0, i)),
            pl.BlockSpec((tile, width), lambda i: (i, 0)),
        ],
        out_specs=(
            pl.BlockSpec((slot_total, tile), lambda i: (0, i)),
            pl.BlockSpec((tile, width), lambda i: (i, 0)),
        ),
        compiler_params=pltpu.CompilerParams(vmem_limit_bytes=24 * 1024 * 1024),
        name="experts",
    )(flat_rows, saved.reshape(-1, ff), down_w[0])
    return (
        section_dx[None],
        jnp.swapaxes(router_grad, 0, 1)[None],
        hidden_grad.reshape(saved.shape)[None],
        down_grad[None],
    )


def solution(mesh):
    placed = (
        P(None, "expert", None),
        P("section", None, "expert", None),
        P("section", None, "expert", None, None),
        P("section", None, None),
        P("section", None, "expert", None),
        P("section", None, None, "expert"),
        P("section", "expert", None),
    )
    return jax.shard_map(
        per_device,
        mesh=mesh,
        in_specs=placed,
        out_specs=(
            P("section", None, "expert", None),
            P("section", None, None),
            P("section", None, None, "expert"),
            P("section", "expert", None),
        ),
        check_vma=False,
    )
```

time: 138 us -> 37 us (0.27); the launches traced: 136 us -> 36.7 us
  matrix products: 45.1 us -> 0 us
  waiting for transfers between devices: 37.2 us -> 0 us
  Pallas kernels: 0 us -> 26.5 us
  blocking collectives: 14.3 us -> 0 us
  between operations: 14.2 us -> 0.66 us
  starting transfers between devices: 10.4 us -> 0 us
  local copies, waits for them, and re-layouts: 12.5 us -> 9.57 us
  other arithmetic: 2.4 us -> 0 us
    dot_general x28 -> x0, matrix products: 45.1 us -> none  [the longest x8 12.8 us: backprop(): jnp.einsum('mtkd,mtd->mtk', outputs, cotangent, preferred_element_type=jn...]
    ppermute x8 -> x0, waiting for transfers between devices: 29.3 us -> none  [passed_along(): return lax.ppermute(value, axis, pairs)]
    pallas_call x0 -> x2, Pallas kernels: none -> 26.5 us  [the longest x1 19.6 us: per_device(): pl.pallas_call(functools.partial(chain_kernel, sections, parts), out_shap...]
    all_gather x1 -> x0, blocking collectives: 14.3 us -> none  [per_device(): gathered = lax.all_gather(rows_out, 'expert', axis=1, tiled=True)]
    ppermute x8 -> x0, starting transfers between devices: 10.3 us -> none  [passed_along(): return lax.ppermute(value, axis, pairs)]
    psum x1 -> x0, waiting for transfers between devices: 7.93 us -> none  [per_device(): router_grad = lax.psum(router_acc, 'expert') / total_tokens]
    unnamed x9 -> x16, local copies, waits for them, and re-layouts: 11.1 us -> 9.57 us
    broadcast_in_dim x1 -> x0, other arithmetic: 1.47 us -> none  [per_device(): router_grad[None]]
  transfers between devices with their start and end apart: 9 -> 0, of which waited for: 9 -> 0; matrix products, arithmetic and copies ran while one was open for 23% -> 0% of each run, Pallas kernels for 0% -> 0%
where the time goes in v1:
time: 37 us; the launch traced here: 36.7 us
  Pallas kernels  26.5 us (72%)
  local copies, waits for them, and re-layouts  9.57 us (26%)
  between operations  0.66 us (2%)
    pallas_call x1, Pallas kernels, per_device(): pl.pallas_call(functools.partial(chain_kernel, sections, parts), out_shap...  19.6 us
    unnamed x16, local copies, waits for them, and re-layouts  9.57 us
    pallas_call x1, Pallas kernels, per_device(): pl.pallas_call(expert_kernel, grid=(ff // tile,), out_shape=(jax.ShapeDty...  6.85 us

profile of v1, /device:TPU:0, one launch (start us, length us, event | category | flops | bytes accessed | tf_op | source)
XLA Modules:
  0.0 36.7 jit_solution(3779848461642354739)
XLA Ops:
  0.6 0.0 copy-start.2
  0.6 0.9 %copy-done.2 = bf16[1,2,16,2,2048]{4,3,2,1,0:T(2,128)(2,1)S(1)} copy-done((bf16[1,2,16,2,2048]{4,3,2,1,0:T(2,128)(2,1)S(1)}, bf16[1,2,16,2,2048]{4,3,2,1,0:T(2,128)(2,1)}, u32[]{:S(2)}) %copy-start.2) | copy-done | bytes 262168
  1.6 0.0 copy-start.3
  1.6 0.9 %copy-done.3 = bf16[2,16,2048]{2,1,0:T(8,128)(2,1)S(1)} copy-done((bf16[2,16,2048]{2,1,0:T(8,128)(2,1)S(1)}, bf16[2,16,2048]{2,1,0:T(8,128)(2,1)}, u32[]{:S(2)}) %copy-start.3) | copy-done | bytes 131096
  2.5 0.0 copy-start.4
  2.5 0.9 %copy-done.4 = bf16[1,2,16,2048]{3,2,1,0:T(8,128)(2,1)S(1)} copy-done((bf16[1,2,16,2048]{3,2,1,0:T(8,128)(2,1)S(1)}, bf16[1,2,16,2048]{3,2,1,0:T(8,128)(2,1)}, u32[]{:S(2)}) %copy-start.4) | copy-done | bytes 131096
  3.4 0.0 copy-start.5
  3.4 0.8 %copy-done.5 = f32[1,2048,8]{1,2,0:T(8,128)S(1)} copy-done((f32[1,2048,8]{1,2,0:T(8,128)S(1)}, f32[1,2048,8]{1,2,0:T(8,128)}, u32[]{:S(2)}) %copy-start.5) | copy-done | bytes 65560
  4.2 0.0 copy-start.6
  4.2 0.7 %copy-done.6 = s32[1,2,16,2]{2,3,1,0:T(2,128)S(1)} copy-done((s32[1,2,16,2]{2,3,1,0:T(2,128)S(1)}, s32[1,2,16,2]{2,3,1,0:T(2,128)}, u32[]{:S(2)}) %copy-start.6) | copy-done | bytes 280
  4.9 19.6 %chain.1 = (bf16[2,16,2048]{2,1,0:T(8,128)(2,1)S(1)}, f32[8,2048]{1,0:T(8,128)S(1)}, bf16[2,32,2048]{2,1,0:T(8,128)(2,1)S(1)}) custom-call(bf16[2,16,2048]{2,1,0:T(8,128)(2,1)S(1)} %copy-done.3, bf16[2,16,2048]{2,1,0:T(8,128)(2,1)S(1)} %bitcast.23, bf16[32,2,2048]{2,1,0:T(2,128)(2,1)S(1)} %bitcast.22, f32[8,2048]{1,0:T(8,128)S(1)} %bitcast.24, ...), custom_call_target="tpu_custom_call" | custom-call | flops 1000000000 | bytes 40000000 | tf_op jit(solution)/shard_map/chain/pallas_call | solution.py:234
  24.5 0.0 copy-start
  24.5 3.1 %copy-done = bf16[1,1792,2048]{2,1,0:T(8,128)(2,1)S(1)} copy-done((bf16[1,1792,2048]{2,1,0:T(8,128)(2,1)S(1)}, bf16[1,1792,2048]{2,1,0:T(8,128)(2,1)}, u32[]{:S(2)}) %copy-start) | copy-done | bytes 7340056
  27.6 0.0 copy-start.1
  27.6 0.9 %copy-done.1 = bf16[1,2,32,1792]{3,2,1,0:T(8,128)(2,1)S(1)} copy-done((bf16[1,2,32,1792]{3,2,1,0:T(8,128)(2,1)S(1)}, bf16[1,2,32,1792]{3,2,1,0:T(8,128)(2,1)}, u32[]{:S(2)}) %copy-start.1) | copy-done | bytes 229400
  28.6 6.9 %experts.1 = (bf16[64,1792]{1,0:T(8,128)(2,1)}, bf16[1792,2048]{1,0:T(8,128)(2,1)}) custom-call(bf16[64,2048]{1,0:T(8,128)(2,1)S(1)} %bitcast.18, bf16[64,1792]{1,0:T(8,128)(2,1)S(1)} %bitcast.19, bf16[1792,2048]{1,0:T(8,128)(2,1)S(1)} %bitcast.17), custom_call_target="tpu_custom_call" | custom-call | tf_op jit(solution)/shard_map/experts/pallas_call | solution.py:282
  35.4 0.7 %copy.13 = bf16[1,2,16,2048]{3,2,1,0:T(8,128)(2,1)} copy(bf16[1,2,16,2048]{3,2,1,0:T(8,128)(2,1)S(1)} %bitcast.20) | data formatting | bytes 262144
  36.1 0.6 %copy.14 = f32[1,2048,8]{1,2,0:T(8,128)} copy(f32[1,2048,8]{1,2,0:T(8,128)S(1)} %bitcast.21) | data formatting | bytes 131072
Async XLA Ops:
  0.6 1.0 %copy-start.2 = (bf16[1,2,16,2,2048]{4,3,2,1,0:T(2,128)(2,1)S(1)}, bf16[1,2,16,2,2048]{4,3,2,1,0:T(2,128)(2,1)}, u32[]{:S(2)}) copy-start(bf16[1,2,16,2,2048]{4,3,2,1,0:T(2,128)(2,1)} %param.9) | copy-start | bytes 786436
  1.6 0.9 %copy-start.3 = (bf16[2,16,2048]{2,1,0:T(8,128)(2,1)S(1)}, bf16[2,16,2048]{2,1,0:T(8,128)(2,1)}, u32[]{:S(2)}) copy-start(bf16[2,16,2048]{2,1,0:T(8,128)(2,1)} %top_ref.1) | copy-start | bytes 393220
  2.5 0.9 %copy-start.4 = (bf16[1,2,16,2048]{3,2,1,0:T(8,128)(2,1)S(1)}, bf16[1,2,16,2048]{3,2,1,0:T(8,128)(2,1)}, u32[]{:S(2)}) copy-start(bf16[1,2,16,2048]{3,2,1,0:T(8,128)(2,1)} %param.8) | copy-start | bytes 393220
  3.4 0.8 %copy-start.5 = (f32[1,2048,8]{1,2,0:T(8,128)S(1)}, f32[1,2048,8]{1,2,0:T(8,128)}, u32[]{:S(2)}) copy-start(f32[1,2048,8]{1,2,0:T(8,128)} %param.10) | copy-start | bytes 196612
  4.2 0.7 %copy-start.6 = (s32[1,2,16,2]{2,3,1,0:T(2,128)S(1)}, s32[1,2,16,2]{2,3,1,0:T(2,128)}, u32[]{:S(2)}) copy-start(s32[1,2,16,2]{2,3,1,0:T(2,128)} %param.11) | copy-start | bytes 772
  24.5 3.1 %copy-start = (bf16[1,1792,2048]{2,1,0:T(8,128)(2,1)S(1)}, bf16[1,1792,2048]{2,1,0:T(8,128)(2,1)}, u32[]{:S(2)}) copy-start(bf16[1,1792,2048]{2,1,0:T(8,128)(2,1)} %param.13) | copy-start | bytes 22020100
  27.6 0.9 %copy-start.1 = (bf16[1,2,32,1792]{3,2,1,0:T(8,128)(2,1)S(1)}, bf16[1,2,32,1792]{3,2,1,0:T(8,128)(2,1)}, u32[]{:S(2)}) copy-start(bf16[1,2,32,1792]{3,2,1,0:T(8,128)(2,1)} %param.12) | copy-start | bytes 688132

commit v2 on v1

--- a/solution.py
+++ b/solution.py
@@ -10,6 +10,10 @@
 F32 = jnp.float32
 BF16 = jnp.bfloat16
 MESH = pl.DeviceIdType.MESH
+
+
+def cuts_of(size):
+    return next(n for n in range(1, size + 1) if size % n == 0 and size // n <= 256)
 
 
 def iota(shape, axis):
@@ -34,14 +38,28 @@
 def chain_kernel(
     sections,
     parts,
+    top_hbm,
+    x_hbm,
+    outs_hbm,
+    w_hbm,
+    ids_hbm,
+    hidden_hbm,
+    down_hbm,
+    dx_ref,
+    router_ref,
+    rows_ref,
+    turned_ref,
+    hidden_out,
+    early_ref,
     top_ref,
     x_ref,
     outs_ref,
     w_ref,
     ids_ref,
-    dx_ref,
-    router_ref,
-    rows_ref,
+    hidden_ref,
+    down_ref,
+    wall_down,
+    load_sem,
     wsend,
     wbuf,
     tsend,
@@ -74,6 +92,24 @@
     all_rows = sections * experts
     pad = msend.shape[1] - all_rows
 
+    loads = {}
+
+    def load(name, src, dst):
+        loads[name] = pltpu.make_async_copy(src, dst, load_sem.at[len(loads)])
+        loads[name].start()
+
+    load("w", w_hbm, w_ref)
+    load("ids", ids_hbm, ids_ref)
+    load("top", top_hbm, top_ref)
+    load("x", x_hbm, x_ref)
+    load("outs", outs_hbm, outs_ref)
+    load("hidden", hidden_hbm, hidden_ref)
+    cuts = cuts_of(down_ref.shape[0])
+    depth = down_ref.shape[0] // cuts
+    for i in range(cuts):
+        cut = pl.ds(i * depth, depth)
+        load(i, down_hbm.at[cut], down_ref.at[cut])
+
     barrier = pltpu.get_barrier_semaphore()
     for i in range(1, sections):
         pl.semaphore_signal(
@@ -84,6 +120,8 @@
             barrier, inc=1, device_id={"expert": (spot + i) % parts}, device_id_type=MESH
         )
 
+    loads["w"].wait()
+    loads["ids"].wait()
     weights = w_ref[...]
     high = weights.astype(BF16)
     low = weights - high.astype(F32)
@@ -114,7 +152,17 @@
             source = (mine + i) % count
             push(src, buf.at[source], out_sem.at[i], in_sem.at[source], axis, source).wait_recv()
 
-    spread(wsend, wbuf, w_out, w_in, "section", me, sections)
+    partner = me + 1 - 2 * (me % 2)
+    pairs = sections // 2
+
+    def weight_push(i, src, slot, target):
+        return push(src, wbuf.at[slot], w_out.at[i], w_in.at[slot], "section", target)
+
+    for i in range(1, pairs):
+        sends.append(weight_push(i, wsend, me, (me + 2 * i) % sections))
+        sends[-1].start()
+    sends.append(weight_push(0, wsend, me, partner))
+    sends[-1].start()
 
     sel = sel_wide[:, :tokens]
     first = sel[0:1, :]
@@ -130,12 +178,14 @@
         & (spots.astype(jnp.int32) == slot_row % cap)
         & (routed > 0.5)
     ).astype(F32)
+    loads["top"].wait()
     top = top_ref[...].reshape(tokens, width)
     top_rows = dot(slot_table.astype(BF16), top).astype(BF16)
     tsend[...] = top_rows
     tbuf[spot] = top_rows
     spread(tsend, tbuf, t_out, t_in, "expert", spot, parts)
 
+    loads["x"].wait()
     x = x_ref[...].reshape(tokens, width)
     both = jnp.concatenate([high.astype(F32), low], axis=0).astype(BF16)
     logits = dot(both, x, ((1,), (1,)))
@@ -145,11 +195,22 @@
     gate_zero = jnp.where(first > 0.5, gate, 1.0 - gate)
     gated_table = slot_table * gate_zero
 
+    loads["outs"].wait()
     diff = (outs_ref[:, 0, :].astype(F32) - outs_ref[:, 1, :].astype(F32)).astype(BF16)
     eye = (iota((tokens, tokens), 0) == iota((tokens, tokens), 1)).astype(F32)
     base = jnp.sum(dot(top, diff, ((1,), (1,))) * eye, axis=0, keepdims=True)
 
-    collect(wsend, wbuf, w_out, w_in, "section", me, sections)
+    loads["hidden"].wait()
+    turned_ref[...] = hidden_ref[...].T
+
+    for i in range(1, pairs):
+        slot = (me + 2 * i) % sections
+        weight_push(i, wsend, slot, slot).wait_recv()
+        sends.append(weight_push(pairs + i, wbuf.at[slot], slot, partner))
+        sends[-1].start()
+    for i in range(pairs):
+        slot = (partner + 2 * i) % sections
+        weight_push(i, wsend, slot, partner).wait_recv()
     wall = jnp.concatenate(
         [wbuf[k, :, :width].astype(F32) for k in range(sections)], axis=0
     ).astype(BF16)
@@ -196,14 +257,37 @@
     dx_ref[...] = moved.astype(BF16).reshape(dx_ref.shape)
 
     collect(tsend, tbuf, t_out, t_in, "expert", spot, parts)
+    tops = jnp.concatenate([tbuf[e].astype(F32) for e in range(parts)], axis=0)
+    sources = jnp.concatenate([wall, tops.astype(BF16)], axis=0)
+    top_down = []
+    for i in range(cuts):
+        loads[i].wait()
+        moved_down = dot(sources, down_ref[i * depth : (i + 1) * depth, :], ((1,), (1,)))
+        wall_down[:, i * depth : (i + 1) * depth] = moved_down[:all_rows].astype(BF16)
+        top_down.append(moved_down[all_rows:])
     collect(msend, mbuf, m_out, m_in, "expert", spot, parts)
-    for e in range(parts):
-        mixed = mbuf[e]
-        part = dot(mixed[:, :all_rows].astype(BF16), wall)
-        part = part + mixed[:, all_rows : all_rows + 1] * tbuf[e].astype(F32)
-        for m in range(micro):
-            rows_ref[m, e * cap : (e + 1) * cap, :] = part[m * cap : (m + 1) * cap].astype(BF16)
-
+    mixed = jnp.concatenate([mbuf[e] for e in range(parts)], axis=0)
+    mixed_rows = mixed[:, :all_rows].astype(BF16)
+    mixed_gate = mixed[:, all_rows : all_rows + 1]
+
+    def place_rows(out, value, columns):
+        for e in range(parts):
+            for m in range(micro):
+                block = value[e * slots + m * cap : e * slots + (m + 1) * cap]
+                at = m * parts * cap + e * cap
+                out[at : at + cap, columns] = block.astype(BF16)
+
+    place_rows(rows_ref, dot(mixed_rows, wall) + mixed_gate * tops, slice(None))
+    for i in range(cuts):
+        columns = slice(i * depth, (i + 1) * depth)
+        value = dot(mixed_rows, wall_down[:, columns]) + mixed_gate * top_down[i]
+        place_rows(hidden_out, value, columns)
+
+    early_rows = rows_ref[...]
+    tile = early_ref.shape[0] // cuts_of(early_ref.shape[0])
+    for i in range(early_ref.shape[0] // tile):
+        cut = pl.ds(i * tile, tile)
+        early_ref[cut, :] = dot(turned_ref[cut, :], early_rows).astype(BF16)
     collect(psend, pbuf, p_out, p_in, "expert", spot, parts)
     total = share
     for i in range(1, parts):
@@ -213,10 +297,40 @@
         copy.wait_send()
 
 
-def expert_kernel(rows_ref, hidden_ref, weight_ref, hidden_out, weight_out):
+def expert_kernel(
+    dx_ref,
+    router_ref,
+    hidden_ref,
+    rows_ref,
+    turned_ref,
+    early_ref,
+    dx_out,
+    router_out,
+    hidden_out,
+    weight_out,
+    product,
+    sem,
+):
+    copies = []
+
+    def store(src, dst):
+        copies.append(pltpu.make_async_copy(src, dst, sem.at[len(copies)]))
+        copies[-1].start()
+
+    done = early_ref.shape[0]
+    tile = weight_out.shape[0] // cuts_of(weight_out.shape[0])
+    for at in range(0, done, tile):
+        store(early_ref.at[pl.ds(at, tile)], weight_out.at[pl.ds(at, tile)])
+    store(dx_ref, dx_out)
+    store(router_ref, router_out)
+    store(hidden_ref, hidden_out)
     rows = rows_ref[...]
-    hidden_out[...] = dot(rows, weight_ref[...], ((1,), (1,))).astype(BF16)
-    weight_out[...] = dot(hidden_ref[...], rows, ((0,), (0,))).astype(BF16)
+    for at in range(done, weight_out.shape[0], tile):
+        cut = pl.ds(at - done, tile)
+        product[cut, :] = dot(turned_ref[pl.ds(at, tile), :], rows).astype(BF16)
+        store(product.at[cut], weight_out.at[pl.ds(at, tile)])
+    for copy in copies:
+        copy.wait()
 
 
 def per_device(top_grad, layer_input, expert_out, router_w, expert_ids, hidden, down_w):
@@ -230,17 +344,35 @@
     lanes = -(-tokens // 128) * 128
     mix_lanes = (sections * experts // 128 + 1) * 128
     vmem = pl.BlockSpec(memory_space=pltpu.VMEM)
+    hbm = pl.BlockSpec(memory_space=pltpu.HBM)
     dma = pltpu.SemaphoreType.DMA
-    section_dx, router_grad, rows = pl.pallas_call(
+    slot_total, ff = parts * slots, down_w.shape[1]
+    cuts = cuts_of(ff)
+    saved = hidden[0].reshape(slot_total, ff)
+    shapes = (
+        jax.ShapeDtypeStruct((micro, tok, width), BF16),
+        jax.ShapeDtypeStruct((experts, width), F32),
+        jax.ShapeDtypeStruct((slot_total, ff), BF16),
+        jax.ShapeDtypeStruct((slot_total, width), BF16),
+        jax.ShapeDtypeStruct((ff, slot_total), BF16),
+    )
+    early = ff // cuts * max(1, cuts * 2 // 8)
+    section_dx, router_grad, rows, turned, hidden_grad, early_grad = pl.pallas_call(
         functools.partial(chain_kernel, sections, parts),
-        out_shape=(
-            jax.ShapeDtypeStruct((micro, tok, width), BF16),
-            jax.ShapeDtypeStruct((experts, width), F32),
-            jax.ShapeDtypeStruct((micro, parts * cap, width), BF16),
-        ),
-        in_specs=[vmem] * 5,
-        out_specs=(vmem,) * 3,
+        out_shape=(shapes[0], shapes[1], shapes[3], shapes[4], shapes[2])
+        + (jax.ShapeDtypeStruct((early, width), BF16),),
+        in_specs=[hbm] * 7,
+        out_specs=(vmem,) * 6,
         scratch_shapes=[
+            pltpu.VMEM((micro, tok, width), BF16),
+            pltpu.VMEM((micro, tok, width), BF16),
+            pltpu.VMEM((tokens, 2, width), BF16),
+            pltpu.VMEM((experts, width), F32),
+            pltpu.VMEM((micro, 2, tok), jnp.int32),
+            pltpu.VMEM((slot_total, ff), BF16),
+            pltpu.VMEM((ff, width), BF16),
+            pltpu.VMEM((sections * experts, ff), BF16),
+            dma((6 + cuts,)),
             pltpu.VMEM((experts, width + lanes), BF16),
             pltpu.VMEM((sections, experts, width + lanes), BF16),
             pltpu.VMEM((slots, width), BF16),
@@ -263,45 +395,37 @@
             dma((parts,)),
         ],
         compiler_params=pltpu.CompilerParams(
-            collective_id=0, has_side_effects=True, vmem_limit_bytes=24 * 1024 * 1024
+            collective_id=0, has_side_effects=True, vmem_limit_bytes=32 * 1024 * 1024
         ),
         cost_estimate=pl.CostEstimate(flops=10**9, bytes_accessed=4 * 10**7, transcendentals=0),
         name="chain",
     )(
-        top_grad,
-        layer_input[0],
-        expert_out[0].reshape(tokens, 2, width),
-        jnp.swapaxes(router_w[0], 0, 1),
-        jnp.swapaxes(expert_ids[0], 1, 2),
-    )
-    flat_rows = rows.reshape(-1, width)
-    saved = hidden[0]
-    ff = down_w.shape[1]
-    slot_total = flat_rows.shape[0]
-    tile = 256 if ff % 256 == 0 else (128 if ff % 128 == 0 else ff)
-    hidden_grad, down_grad = pl.pallas_call(
+        *[
+            pltpu.with_memory_space_constraint(value, pltpu.HBM)
+            for value in (
+                top_grad,
+                layer_input[0],
+                expert_out[0].reshape(tokens, 2, width),
+                jnp.swapaxes(router_w[0], 0, 1),
+                jnp.swapaxes(expert_ids[0], 1, 2),
+                saved,
+                down_w[0],
+            )
+        ]
+    )
+    section_dx, router_grad, hidden_grad, down_grad = pl.pallas_call(
         expert_kernel,
-        grid=(ff // tile,),
-        out_shape=(
-            jax.ShapeDtypeStruct((slot_total, ff), BF16),
-            jax.ShapeDtypeStruct((ff, width), BF16),
-        ),
-        in_specs=[
-            pl.BlockSpec((slot_total, width), lambda i: (0, 0)),
-            pl.BlockSpec((slot_total, tile), lambda i: (0, i)),
-            pl.BlockSpec((tile, width), lambda i: (i, 0)),
-        ],
-        out_specs=(
-            pl.BlockSpec((slot_total, tile), lambda i: (0, i)),
-            pl.BlockSpec((tile, width), lambda i: (i, 0)),
-        ),
-        compiler_params=pltpu.CompilerParams(vmem_limit_bytes=24 * 1024 * 1024),
+        out_shape=(shapes[0], shapes[1], shapes[2], jax.ShapeDtypeStruct((ff, width), BF16)),
+        in_specs=[vmem] * 6,
+        out_specs=(hbm,) * 4,
+        scratch_shapes=[pltpu.VMEM((ff - early, width), BF16), dma((3 + cuts,))],
+        compiler_params=pltpu.CompilerParams(vmem_limit_bytes=32 * 1024 * 1024),
         name="experts",
-    )(flat_rows, saved.reshape(-1, ff), down_w[0])
+    )(section_dx, router_grad, hidden_grad, rows, turned, early_grad)
     return (
         section_dx[None],
         jnp.swapaxes(router_grad, 0, 1)[None],
-        hidden_grad.reshape(saved.shape)[None],
+        hidden_grad.reshape(hidden.shape),
         down_grad[None],
     )
 

time: 37 us -> 24 us (0.65)
  local copies, waits for them, and re-layouts: 9.57 us -> 0 us
  Pallas kernels: 26.5 us -> 23.2 us
    unnamed x16 -> x0, local copies, waits for them, and re-layouts: 9.57 us -> none
    pallas_call x1, Pallas kernels: 6.85 us -> 3.21 us  [per_device(): pl.pallas_call(expert_kernel, out_shape=(shapes[0], shapes[1], shapes[2],...]
    pallas_call x1, Pallas kernels: 19.6 us -> 20 us  [per_device(): pl.pallas_call(functools.partial(chain_kernel, sections, parts), out_shap...]
where the time goes in v2:
time: 24 us; the launch traced here: 23.9 us
  Pallas kernels  23.2 us (97%)
  between operations  0.64 us (3%)
    pallas_call x1, Pallas kernels, per_device(): pl.pallas_call(functools.partial(chain_kernel, sections, parts), out_shap...  20 us
    pallas_call x1, Pallas kernels, per_device(): pl.pallas_call(expert_kernel, out_shape=(shapes[0], shapes[1], shapes[2],...  3.21 us

profile of v2, /device:TPU:0, one launch (start us, length us, event | category | flops | bytes accessed | tf_op | source)
XLA Modules:
  0.0 23.9 jit_solution(7857517619400798231)
XLA Ops:
  0.6 20.0 %chain.1 = (bf16[2,16,2048]{2,1,0:T(8,128)(2,1)S(1)}, f32[8,2048]{1,0:T(8,128)S(1)}, bf16[64,2048]{1,0:T(8,128)(2,1)S(1)}, bf16[1792,64]{1,0:T(8,128)(2,1)S(1)},...) custom-call(bf16[2,16,2048]{2,1,0:T(8,128)(2,1)} %top_hbm.1, bf16[2,16,2048]{2,1,0:T(8,128)(2,1)} %bitcast.19, ...), custom_call_target="tpu_custom_call" | custom-call | flops 1000000000 | bytes 40000000 | tf_op jit(solution)/shard_map/chain/pallas_call | solution.py:360
  20.7 3.2 %experts.1 = (bf16[2,16,2048]{2,1,0:T(8,128)(2,1)}, f32[8,2048]{1,0:T(8,128)}, bf16[64,1792]{1,0:T(8,128)(2,1)}, bf16[1792,2048]{1,0:T(8,128)(2,1)}) custom-call(bf16[2,16,2048]{2,1,0:T(8,128)(2,1)S(1)} %get-tuple-element.14.dx_ref, f32[8,2048]{1,0:T(8,128)S(1)} %get-tuple-element.15.router_ref, bf16[64,1792]{1,0:T(8,128)(2,1)S(1)} %get-tuple-element.16.hidden_ref, ...), custom_call_target="tpu_custom_call" | custom-call | tf_op jit(solution)/shard_map/experts/pallas_call | solution.py:416
